TPU v7x, 32 devices: a whole 2x2x4 slice. The times are simulated.
32 devices in a mesh: dp: 4 (over x, core), fsdp: 2 (over y), tensor: 4 (over z).
Axes of the slice: x: 2, y: 2, z: 4, core: 2. Of those that a mesh axis runs over, the one named last changes fastest.
Arguments:
- tokens: bfloat16 [8, 768, 8192], P(('dp', 'fsdp'), 'tensor'), may hold values from -6 to 6
- norm_gain: float32 [8192], replicated, may hold values from 0.85 to 4
- w_qkv: bfloat16 [8192, 5120], P(('dp', 'fsdp'), 'tensor'), may hold values from -0.3 to 0.3
- a_query: bfloat16 [8192, 16], replicated, may hold values from -0.0625 to 0.0625
- query_up_adapter: bfloat16 [16, 4096], P(None, 'tensor'), may hold values from -1.5 to 1.5
- a_value: bfloat16 [8192, 16], replicated, may hold values from -0.0625 to 0.0625
- value_up_adapter: bfloat16 [16, 512], P(None, 'tensor'), may hold values from -1.5 to 1.5
- out_grad: bfloat16 [8, 768, 4096], P(('dp', 'fsdp'), 'tensor'), may hold values from -6 to 6
Outputs:
- attn_out: bfloat16 [8, 768, 4096], P(('dp', 'fsdp'), 'tensor')
- grad_a_query: float32 [8192, 16], replicated
- grad_b_query: float32 [16, 4096], P(None, 'tensor')
- grad_a_value: float32 [8192, 16], replicated
- grad_b_value: float32 [16, 512], P(None, 'tensor')
All inputs are finite; a program needn't handle non-finite values.
Results may differ from a plain program's by a relative error of at most 0.015.
The roundings to bfloat16 on the way count: a program that leaves them out, or rounds other values in their place, can miss the bound.
Values may be sent and summed in bfloat16 or wider, within the bound.
A program may use at most 256 MiB of HBM per device.

v0:
```python
import math
import jax
import jax.numpy as jnp
from jax import lax
from jax.sharding import PartitionSpec as P

HD = 128
QUERY_PER_KV = 8
EPSILON = 1e-05
ADAPTER_SCALE = 2.0
ROPE_BASE = 500000.0


def normalize(own_rows, norm_gain):
    widened = own_rows.astype(jnp.float32)
    mean_square = jnp.mean(widened * widened, axis=-1, keepdims=True)
    return (widened * lax.rsqrt(mean_square + EPSILON) * norm_gain).astype(jnp.bfloat16)


def rotary(heads_block):
    sequence_length = heads_block.shape[0]
    half_dim = heads_block.shape[-1] // 2
    positions = jnp.arange(sequence_length, dtype=jnp.float32)[:, None]
    inv_freq = ROPE_BASE ** (-jnp.arange(half_dim, dtype=jnp.float32) / half_dim)
    angles = positions * inv_freq
    cosine = jnp.cos(angles)[:, None, :]
    sine_table = jnp.sin(angles)[:, None, :]
    front_half = heads_block[..., :half_dim].astype(jnp.float32)
    back_half = heads_block[..., half_dim:].astype(jnp.float32)
    turned = jnp.concatenate(
        [
            front_half * cosine - back_half * sine_table,
            back_half * cosine + front_half * sine_table,
        ],
        -1,
    )
    return turned.astype(jnp.bfloat16)


def attend(query_rows, key_heads, value_rows):
    sequence_length = query_rows.shape[0]
    kv_heads = key_heads.shape[1] // HD
    rot_queries = rotary(query_rows.reshape(sequence_length, kv_heads * QUERY_PER_KV, HD))
    rot_keys = rotary(key_heads.reshape(sequence_length, kv_heads, HD))
    split_values = value_rows.reshape(sequence_length, kv_heads, HD)
    causal = jnp.arange(sequence_length)[:, None] >= jnp.arange(sequence_length)[None, :]

    def one_head(head_index):
        q_head = lax.dynamic_index_in_dim(rot_queries, head_index, 1, keepdims=False)
        k_head = lax.dynamic_index_in_dim(rot_keys, head_index // QUERY_PER_KV, 1, keepdims=False)
        v_head = lax.dynamic_index_in_dim(
            split_values, head_index // QUERY_PER_KV, 1, keepdims=False
        )
        scores = jnp.dot(q_head, k_head.T, preferred_element_type=jnp.float32) * (
            1.0 / math.sqrt(HD)
        )
        scores = jnp.where(causal, scores, -1e30)
        row_max = jnp.max(scores, axis=-1, keepdims=True)
        weights = jnp.exp(scores - row_max)
        probabilities = (weights / jnp.sum(weights, axis=-1, keepdims=True)).astype(jnp.bfloat16)
        return jnp.dot(probabilities, v_head, preferred_element_type=jnp.float32).astype(
            jnp.bfloat16
        )

    per_head = lax.map(one_head, jnp.arange(kv_heads * QUERY_PER_KV, dtype=jnp.int32))
    return jnp.transpose(per_head, (1, 0, 2)).reshape(sequence_length, kv_heads * QUERY_PER_KV * HD)


def local(tokens, norm_gain, w_qkv, a_query, query_up_adapter, a_value, value_up_adapter, out_grad):
    normed_input = normalize(tokens[0], norm_gain)
    gathered = lax.all_gather(normed_input, "tensor", axis=0, tiled=True)
    sequence_length = gathered.shape[0]
    col_count = w_qkv.shape[1]
    projected = jnp.dot(
        gathered,
        lax.all_gather(w_qkv, ("dp", "fsdp"), axis=0, tiled=True),
        preferred_element_type=jnp.float32,
    )
    narrow_rank_rows = a_query.shape[1]
    down_projected = jnp.dot(
        gathered, jnp.concatenate([a_query, a_value], 1), preferred_element_type=jnp.float32
    ).astype(jnp.bfloat16)
    kv_local = col_count // ((QUERY_PER_KV + 2) * HD)
    grouped_queries = projected.reshape(sequence_length, kv_local, QUERY_PER_KV + 2, HD)
    query_rows = (
        grouped_queries[:, :, :QUERY_PER_KV].reshape(sequence_length, -1)
        + ADAPTER_SCALE
        * jnp.dot(
            down_projected[:, :narrow_rank_rows],
            query_up_adapter,
            preferred_element_type=jnp.float32,
        )
    ).astype(jnp.bfloat16)
    key_heads = (
        grouped_queries[:, :, QUERY_PER_KV].reshape(sequence_length, -1).astype(jnp.bfloat16)
    )
    value_rows = (
        grouped_queries[:, :, QUERY_PER_KV + 1].reshape(sequence_length, -1)
        + ADAPTER_SCALE
        * jnp.dot(
            down_projected[:, narrow_rank_rows:],
            value_up_adapter,
            preferred_element_type=jnp.float32,
        )
    ).astype(jnp.bfloat16)
    grad_rows = lax.all_to_all(out_grad[0], "tensor", split_axis=1, concat_axis=0, tiled=True)
    attended, pullback = jax.vjp(attend, query_rows, key_heads, value_rows)
    query_gradient, grad_keys, value_gradient = pullback(grad_rows)
    out_rows = lax.all_to_all(attended, "tensor", split_axis=0, concat_axis=1, tiled=True)
    query_up_gradient = ADAPTER_SCALE * jnp.einsum(
        "fb,fd->bd",
        down_projected[:, :narrow_rank_rows],
        query_gradient,
        preferred_element_type=jnp.float32,
    )
    value_up_gradient = ADAPTER_SCALE * jnp.einsum(
        "fb,fd->bd",
        down_projected[:, narrow_rank_rows:],
        value_gradient,
        preferred_element_type=jnp.float32,
    )
    middle_gradient = jnp.concatenate(
        [
            jnp.dot(query_gradient, query_up_adapter.T, preferred_element_type=jnp.float32),
            jnp.dot(value_gradient, value_up_adapter.T, preferred_element_type=jnp.float32),
        ],
        1,
    )
    mid_summed = lax.psum(middle_gradient, "tensor").astype(jnp.bfloat16)
    down_gradient = ADAPTER_SCALE * jnp.einsum(
        "uh,ux->hx", gathered, mid_summed, preferred_element_type=jnp.float32
    )
    down_gradient, query_up_gradient, value_up_gradient = lax.psum(
        (down_gradient, query_up_gradient, value_up_gradient), ("dp", "fsdp")
    )
    return (
        out_rows[None],
        down_gradient[:, :narrow_rank_rows],
        query_up_gradient,
        down_gradient[:, narrow_rank_rows:],
        value_up_gradient,
    )


def solution(mesh):
    return jax.shard_map(
        local,
        mesh=mesh,
        in_specs=(
            P(("dp", "fsdp"), "tensor", None),
            P(),
            P(("dp", "fsdp"), "tensor"),
            P(),
            P(None, "tensor"),
            P(),
            P(None, "tensor"),
            P(("dp", "fsdp"), "tensor", None),
        ),
        out_specs=(
            P(("dp", "fsdp"), "tensor", None),
            P(),
            P(None, "tensor"),
            P(),
            P(None, "tensor"),
        ),
        check_vma=False,
    )
```

profile of v0, /device:TPU:0, one launch (start us, length us, event | category | flops | bytes accessed | tf_op | source)
XLA Modules:
  0.0 691.3 jit_solution(7818503089707505698)
XLA Ops:
  7.2 2.8 fusion.62
  10.0 3.3 fusion.64
  17.5 6.3 all-to-all-start.1
  25.4 77.7 %all-to-all-done.1 = bf16[192,4,1024]{2,0,1:T(8,128)(2,1)S(1)} async-done(((bf16[192,4,1024]{2,0,1:T(8,128)(2,1)}), bf16[192,4,1024]{2,0,1:T(8,128)(2,1)S(1)}, u32[]{:S(2)}, u32[]{:S(2)}) %all-to-all-start.1) | async-done | bytes 1572896 | tf_op jit(solution)/shard_map/all_to_all | solution.py:106
  105.0 158.8 %all-gather.3.cloned.1.call-done = bf16[768,8192]{1,0:T(8,128)(2,1)} async-done(((bf16[192,8192]{1,0:T(8,128)(2,1)}), bf16[768,8192]{1,0:T(8,128)(2,1)}) %all-gather.3.cloned.1.call-update) | async-done | bytes 12582928 | tf_op jit(solution)/shard_map/all_gather | solution.py:71
  263.8 8.4 %convolution_convert_fusion.2 = bf16[768,32]{0,1:T(8,128)(2,1)S(1)} fusion(bf16[768,8192]{1,0:T(8,128)(2,1)} %all-gather.3.cloned.1.call-done, bf16[8192,16]{0,1:T(8,128)(2,1)S(1)} %copy-done.6, bf16[8192,16]{0,1:T(8,128)(2,1)S(1)} %copy-done.7), kind=kOutput, calls=%fused_computation.94 | convolution fusion | flops 403726336 | bytes 13156352 | tf_op jit(solution)/shard_map/dot_general | solution.py:80
  272.2 100.1 %all-gather.5.cloned.1.call-done = bf16[8192,1280]{1,0:T(8,128)(2,1)} async-done(((bf16[1024,1280]{1,0:T(8,128)(2,1)}), bf16[8192,1280]{1,0:T(8,128)(2,1)}) %all-gather.5.cloned.1.call-update) | async-done | bytes 20971536 | tf_op jit(solution)/shard_map/all_gather | solution.py:76
  372.3 22.9 %fusion.95 = f32[768,1280]{0,1:T(8,128)S(1)} fusion(bf16[768,8192]{1,0:T(8,128)(2,1)} %all-gather.3.cloned.1.call-done, bf16[8192,1280]{1,0:T(8,128)(2,1)} %all-gather.5.cloned.1.call-done), kind=kOutput, calls=%fused_computation.131 | convolution fusion | flops 16106127360 | bytes 37486592 | tf_op jit(solution)/shard_map/dot_general | solution.py:74
  407.8 85.5 %while.52 = (s32[]{:T(128)}, bf16[8,768,128]{2,1,0:T(8,128)(2,1)}, s32[8]{0:T(128)S(1)}, bf16[8,128,768]{2,1,0:T(8,128)(2,1)}, f32[8,768,768]{1,2,0:T(8,128)}, /...) while((s32[]{:T(128)}, bf16[8,768,128]{2,1,0:T(8,128)(2,1)}, ...), condition=%wide.region_5.6_spmd.clone, body=%wide.region_1.5_spmd.clone.sunk | while | flops 310344960 | bytes 20494060 | solution.py:65
  465.1 2.6 fusion.126
  493.5 98.7 %while.53 = (s32[]{:T(128)}, bf16[768,8,128]{0,2,1:T(8,128)(2,1)S(1)}, bf16[768,1,128]{2,0,1:T(8,128)(2,1)}, s32[8]{0:T(128)S(1)}, bf16[8,768,128]{2,1,0:T(8,128...) while((s32[]{:T(128)}, ...), condition=%wide.region_9.10_spmd.clone, body=%wide.region_6.9_spmd.clone.sunk | while | flops 464683776 | bytes 17364168 | solution.py:65
  499.7 3.0 fusion.133
  511.9 3.0 fusion.133
  524.3 3.0 fusion.133
  536.6 3.0 fusion.133
  548.9 3.0 fusion.133
  561.2 3.0 fusion.133
  573.5 3.0 fusion.133
  585.9 3.0 fusion.133
  595.4 20.2 %psum.28 = bf16[768,32]{0,1:T(8,128)(2,1)S(1)} all-reduce(f32[768,32]{0,1:T(8,128)S(1)} %pad_maximum_fusion.2), channel_id=1, replica_groups=mesh['dp'=4,'fsdp'=2,'tensor'=4] {'tensor'}, use_global_device_ids=true, to_apply=%region_10.11 | all-reduce | flops 24576 | bytes 147456 | tf_op jit(solution)/shard_map/psum | solution.py:129
  615.6 7.9 %convolution_multiply_fusion = f32[8192,32]{0,1:T(8,128)} fusion(bf16[768,8192]{1,0:T(8,128)(2,1)} %all-gather.3.cloned.1.call-done, bf16[768,32]{0,1:T(8,128)(2,1)S(1)} %psum.28), kind=kOutput, calls=%fused_computation.71 | convolution fusion | flops 402915328 | bytes 13680640 | tf_op jit(solution)/shard_map/uh,ux->hx/dot_general | solution.py:130
  626.7 3.6 all-to-all-start
  630.4 13.6 %psum.31 = f32[16,128]{1,0:T(8,128)} all-reduce(f32[16,128]{1,0:T(8,128)S(1)} %convolution_multiply_fusion.3), channel_id=1, replica_groups=mesh['dp'=4,'fsdp'=2,'tensor'=4] {'dp','fsdp'}, use_global_device_ids=true, to_apply=%region_13.14 | all-reduce | flops 2048 | bytes 16384 | tf_op jit(solution)/shard_map/psum | solution.py:133
  644.0 34.3 %all-reduce.5.cloned.1.call-done = (f32[8192,32]{0,1:T(8,128)}, f32[16,1024]{1,0:T(8,128)}) async-done(((f32[8192,32]{0,1:T(8,128)}, f32[16,1024]{1,0:T(8,128)}), (f32[8192,32]{0,1:T(8,128)}, f32[16,1024]{1,0:T(8,128)})) %all-reduce.5.cloned.1.call-update) | async-done | bytes 1114128 | tf_op jit(solution)/shard_map/psum | solution.py:133
  (264 shorter events, 174.3 us)
Async XLA Ops:
  7.2 392.2 %copy-start = (bf16[16,1024]{1,0:T(8,128)(2,1)S(1)}, bf16[16,1024]{1,0:T(8,128)(2,1)}, u32[]{:S(2)}) copy-start(bf16[16,1024]{1,0:T(8,128)(2,1)} %param.16) | copy-start | bytes 98308
  7.2 2.8 copy-start.1
  7.2 256.6 %all-gather.3.cloned.1.call-start = ((), (), s32[]{:S(2)}) async-start(), calls=%async_computation.2 | async-start | bytes 15728640 | tf_op jit(solution)/shard_map/all_gather | solution.py:71
  13.3 1.4 copy-start.3
  13.3 359.0 %all-gather.5.cloned.1.call-start = ((), (), s32[]{:S(2)}) async-start(), calls=%async_computation.3 | async-start | bytes 23592960 | tf_op jit(solution)/shard_map/all_gather | solution.py:76
  17.5 85.6 %all-to-all-start.1 = ((bf16[192,4,1024]{2,0,1:T(8,128)(2,1)}), bf16[192,4,1024]{2,0,1:T(8,128)(2,1)S(1)}, u32[]{:S(2)}, u32[]{:S(2)}) async-start(bf16[192,4,1024]{2,0,1:T(8,128)(2,1)} %copy.38), calls=%async_computation.1 | async-start | bytes 3145728 | tf_op jit(solution)/shard_map/all_to_all | solution.py:106
  23.9 654.4 %all-reduce.5.cloned.1.call-start = ((), (), s32[]{:S(2)}) async-start(), calls=%async_computation.4 | async-start | bytes 2228224 | tf_op jit(solution)/shard_map/psum | solution.py:133
  103.6 160.3 %copy-start.6 = (bf16[8192,16]{0,1:T(8,128)(2,1)S(1)}, bf16[8192,16]{0,1:T(8,128)(2,1)}, u32[]{:S(2)}) copy-start(bf16[8192,16]{0,1:T(8,128)(2,1)} %param.17) | copy-start | bytes 786436
  103.6 160.2 %copy-start.7 = (bf16[8192,16]{0,1:T(8,128)(2,1)S(1)}, bf16[8192,16]{0,1:T(8,128)(2,1)}, u32[]{:S(2)}) copy-start(bf16[8192,16]{0,1:T(8,128)(2,1)} %param.15) | copy-start | bytes 786436
  406.9 0.7 copy-start.9
  592.2 0.9 copy-start.2
  593.7 1.5 copy-start.5
  615.6 8.0 %copy-start.4 = (bf16[8,768,128]{2,1,0:T(8,128)(2,1)S(1)}, bf16[8,768,128]{2,1,0:T(8,128)(2,1)}, u32[]{:S(2)}) copy-start(bf16[8,768,128]{2,1,0:T(8,128)(2,1)} %get-tuple-element.648) | copy-start | bytes 4718596
  626.7 53.8 %all-to-all-start = ((bf16[4,192,1024]{2,1,0:T(8,128)(2,1)}), bf16[4,192,1024]{2,1,0:T(8,128)(2,1)S(1)}, u32[]{:S(2)}, u32[]{:S(2)}) async-start(bf16[4,192,1024]{2,1,0:T(8,128)(2,1)} %all_to_all.24), calls=%async_computation | async-start | bytes 3145728 | tf_op jit(solution)/shard_map/all_to_all | solution.py:109
  681.7 2.4 copy-start.8
Sparse Core Ops, SparseCore 0:
  13.4 250.3 all-gather.2
  265.7 106.5 all-gather.4
  623.7 54.5 all-reduce.4
where the time goes:
time: 693 us; the launch traced here: 691 us
  waiting for transfers between devices  372 us (54%)
  matrix products  121 us (17%)
  other arithmetic  66.7 us (10%)
  local copies, waits for them, and re-layouts  57.7 us (8%)
  blocking collectives  33.8 us (5%)
  loops' own time  16.5 us (2%)
  between operations  14.1 us (2%)
  starting transfers between devices  9.99 us (1%)
    all_gather x1, waiting for transfers between devices, local(): gathered = lax.all_gather(normed_input, 'tensor', axis=0, tiled=True)  159 us
    all_gather x1, waiting for transfers between devices, local(): lax.all_gather(w_qkv, ('dp', 'fsdp'), axis=0, tiled=True)  100 us
    all_to_all x1, waiting for transfers between devices, local(): lax.all_to_all(out_grad[0], 'tensor', split_axis=1, concat_axis=0, tiled=...  77.7 us
    dot_general x24, matrix products, one_head(): jnp.dot(probabilities, v_head, preferred_element_type=jnp.float32)  48.5 us
    psum x1, waiting for transfers between devices, local(): lax.psum((down_gradient, query_up_gradient, value_up_gradient), ('dp', 'f...  34.3 us
    dynamic_update_slice x24, other arithmetic, attend(): lax.map(one_head, jnp.arange(kv_heads * QUERY_PER_KV, dtype=jnp.int32))  31.9 us
    dot_general x16, matrix products, one_head(): jnp.dot(q_head, k_head.T, preferred_element_type=jnp.float32)  28.8 us
    dot_general x1, matrix products, local(): jnp.dot(gathered, lax.all_gather(w_qkv, ('dp', 'fsdp'), axis=0, tiled=Tru...  22.9 us
  transfers between devices with their start and end apart: 5, of which 4 were waited for; matrix products, arithmetic and copies ran while one was open for 2% of the time, Pallas kernels for 0%

commit v1 on v0

--- a/solution.py
+++ b/solution.py
@@ -131,7 +131,7 @@
         "uh,ux->hx", gathered, mid_summed, preferred_element_type=jnp.float32
     )
     down_gradient, query_up_gradient, value_up_gradient = lax.psum(
-        (down_gradient, query_up_gradient, value_up_gradient), ("dp", "fsdp")
+        lax.psum((down_gradient, query_up_gradient, value_up_gradient), "fsdp"), "dp"
     )
     return (
         out_rows[None],

time: 693 us -> 720 us (1.039)
  waiting for transfers between devices: 372 us -> 399 us
    psum x1 -> x2, waiting for transfers between devices: 34.3 us -> 58.7 us  [the longest x1 39 us: local(): lax.psum((down_gradient, query_up_gradient, value_up_gradient), 'fsdp')]
  transfers between devices with their start and end apart: 5 -> 6, of which waited for: 4 -> 6; matrix products, arithmetic and copies ran while one was open for 2% -> 2% of each run, Pallas kernels for 0% -> 0%
where the time goes in v1:
time: 720 us; the launch traced here: 718 us
  waiting for transfers between devices  399 us (55%)
  matrix products  121 us (17%)
  other arithmetic  66.7 us (9%)
  local copies, waits for them, and re-layouts  57.8 us (8%)
  blocking collectives  31.9 us (4%)
  loops' own time  16.5 us (2%)
  between operations  14.1 us (2%)
  starting transfers between devices  11.1 us (2%)
    all_gather x1, waiting for transfers between devices, local(): gathered = lax.all_gather(normed_input, 'tensor', axis=0, tiled=True)  159 us
    all_gather x1, waiting for transfers between devices, local(): lax.all_gather(w_qkv, ('dp', 'fsdp'), axis=0, tiled=True)  100 us
    all_to_all x1, waiting for transfers between devices, local(): lax.all_to_all(out_grad[0], 'tensor', split_axis=1, concat_axis=0, tiled=...  77.7 us
    dot_general x24, matrix products, one_head(): jnp.dot(probabilities, v_head, preferred_element_type=jnp.float32)  48.5 us
    psum x1, waiting for transfers between devices, local(): lax.psum((down_gradient, query_up_gradient, value_up_gradient), 'fsdp')  39 us
    dynamic_update_slice x24, other arithmetic, attend(): lax.map(one_head, jnp.arange(kv_heads * QUERY_PER_KV, dtype=jnp.int32))  31.9 us
    dot_general x16, matrix products, one_head(): jnp.dot(q_head, k_head.T, preferred_element_type=jnp.float32)  28.8 us
    dot_general x1, matrix products, local(): jnp.dot(gathered, lax.all_gather(w_qkv, ('dp', 'fsdp'), axis=0, tiled=Tru...  22.9 us
  transfers between devices with their start and end apart: 6, of which 6 were waited for; matrix products, arithmetic and copies ran while one was open for 2% of the time, Pallas kernels for 0%

profile of v1, /device:TPU:0, one launch (start us, length us, event | category | flops | bytes accessed | tf_op | source)
XLA Modules:
  0.0 718.0 jit_solution(17576727535098097877)
XLA Ops:
  10.0 3.3 fusion.64
  17.5 6.3 all-to-all-start.1
  25.4 77.7 %all-to-all-done.1 = bf16[192,4,1024]{2,0,1:T(8,128)(2,1)S(1)} async-done(((bf16[192,4,1024]{2,0,1:T(8,128)(2,1)}), bf16[192,4,1024]{2,0,1:T(8,128)(2,1)S(1)}, u32[]{:S(2)}, u32[]{:S(2)}) %all-to-all-start.1) | async-done | bytes 1572896 | tf_op jit(solution)/shard_map/all_to_all | solution.py:106
  105.0 158.8 %all-gather.3.cloned.1.call-done = bf16[768,8192]{1,0:T(8,128)(2,1)} async-done(((bf16[192,8192]{1,0:T(8,128)(2,1)}), bf16[768,8192]{1,0:T(8,128)(2,1)}) %all-gather.3.cloned.1.call-update) | async-done | bytes 12582928 | tf_op jit(solution)/shard_map/all_gather | solution.py:71
  263.8 8.4 %convolution_convert_fusion.2 = bf16[768,32]{0,1:T(8,128)(2,1)S(1)} fusion(bf16[768,8192]{1,0:T(8,128)(2,1)} %all-gather.3.cloned.1.call-done, bf16[8192,16]{0,1:T(8,128)(2,1)S(1)} %copy-done.6, bf16[8192,16]{0,1:T(8,128)(2,1)S(1)} %copy-done.7), kind=kOutput, calls=%fused_computation.94 | convolution fusion | flops 403726336 | bytes 13156352 | tf_op jit(solution)/shard_map/dot_general | solution.py:80
  272.2 100.1 %all-gather.5.cloned.1.call-done = bf16[8192,1280]{1,0:T(8,128)(2,1)} async-done(((bf16[1024,1280]{1,0:T(8,128)(2,1)}), bf16[8192,1280]{1,0:T(8,128)(2,1)}) %all-gather.5.cloned.1.call-update) | async-done | bytes 20971536 | tf_op jit(solution)/shard_map/all_gather | solution.py:76
  372.3 22.9 %fusion.95 = f32[768,1280]{0,1:T(8,128)S(1)} fusion(bf16[768,8192]{1,0:T(8,128)(2,1)} %all-gather.3.cloned.1.call-done, bf16[8192,1280]{1,0:T(8,128)(2,1)} %all-gather.5.cloned.1.call-done), kind=kOutput, calls=%fused_computation.131 | convolution fusion | flops 16106127360 | bytes 37486592 | tf_op jit(solution)/shard_map/dot_general | solution.py:74
  407.9 85.6 %while.52 = (s32[]{:T(128)}, bf16[8,768,128]{2,1,0:T(8,128)(2,1)}, s32[8]{0:T(128)S(1)}, bf16[8,128,768]{2,1,0:T(8,128)(2,1)}, f32[8,768,768]{1,2,0:T(8,128)}, /...) while((s32[]{:T(128)}, bf16[8,768,128]{2,1,0:T(8,128)(2,1)}, ...), condition=%wide.region_5.6_spmd.clone, body=%wide.region_1.5_spmd.clone.sunk | while | flops 310344960 | bytes 20494060 | solution.py:65
  493.6 98.7 %while.53 = (s32[]{:T(128)}, bf16[768,8,128]{0,2,1:T(8,128)(2,1)S(1)}, bf16[768,1,128]{2,0,1:T(8,128)(2,1)}, s32[8]{0:T(128)S(1)}, bf16[8,768,128]{2,1,0:T(8,128...) while((s32[]{:T(128)}, ...), condition=%wide.region_9.10_spmd.clone, body=%wide.region_6.9_spmd.clone.sunk | while | flops 464683776 | bytes 17364168 | solution.py:65
  499.8 3.0 fusion.133
  512.1 3.0 fusion.133
  524.4 3.0 fusion.133
  536.7 3.0 fusion.133
  549.0 3.0 fusion.133
  561.4 3.0 fusion.133
  573.7 3.0 fusion.133
  586.0 3.0 fusion.133
  595.6 20.2 %psum.49 = bf16[768,32]{0,1:T(8,128)(2,1)S(1)} all-reduce(f32[768,32]{0,1:T(8,128)S(1)} %pad_maximum_fusion.2), channel_id=1, replica_groups=mesh['dp'=4,'fsdp'=2,'tensor'=4] {'tensor'}, use_global_device_ids=true, to_apply=%region_10.11 | all-reduce | flops 24576 | bytes 147456 | tf_op jit(solution)/shard_map/psum | solution.py:129
  615.7 7.9 %convolution_multiply_fusion = f32[8192,32]{0,1:T(8,128)} fusion(bf16[768,8192]{1,0:T(8,128)(2,1)} %all-gather.3.cloned.1.call-done, bf16[768,32]{0,1:T(8,128)(2,1)S(1)} %psum.49), kind=kOutput, calls=%fused_computation.71 | convolution fusion | flops 402915328 | bytes 13680640 | tf_op jit(solution)/shard_map/uh,ux->hx/dot_general | solution.py:130
  623.7 39.0 %all-reduce.9.cloned.1.call-done = (f32[8192,32]{0,1:T(8,128)}, f32[16,1024]{1,0:T(8,128)}) async-done(((f32[8192,32]{0,1:T(8,128)}, f32[16,1024]{1,0:T(8,128)}), (f32[8192,32]{0,1:T(8,128)}, f32[16,1024]{1,0:T(8,128)})) %all-reduce.9.cloned.1.call-update) | async-done | bytes 1114128 | tf_op jit(solution)/shard_map/psum | solution.py:134
  665.8 4.6 all-to-all-start
  670.5 5.0 psum.54
  675.5 6.8 psum.55
  682.3 19.7 %all-reduce.7.cloned.1.call-done = (f32[8192,32]{0,1:T(8,128)}, f32[16,1024]{1,0:T(8,128)}) async-done(((f32[8192,32]{0,1:T(8,128)}, f32[16,1024]{1,0:T(8,128)}), (f32[8192,32]{0,1:T(8,128)}, f32[16,1024]{1,0:T(8,128)})) %all-reduce.7.cloned.1.call-update) | async-done | bytes 1114128 | tf_op jit(solution)/shard_map/psum | solution.py:133
  (268 shorter events, 182.8 us)
Async XLA Ops:
  7.2 392.2 %copy-start = (bf16[16,1024]{1,0:T(8,128)(2,1)S(1)}, bf16[16,1024]{1,0:T(8,128)(2,1)}, u32[]{:S(2)}) copy-start(bf16[16,1024]{1,0:T(8,128)(2,1)} %param.16) | copy-start | bytes 98308
  7.2 2.8 copy-start.1
  7.2 256.6 %all-gather.3.cloned.1.call-start = ((), (), s32[]{:S(2)}) async-start(), calls=%async_computation.2 | async-start | bytes 15728640 | tf_op jit(solution)/shard_map/all_gather | solution.py:71
  13.3 1.4 copy-start.3
  13.3 359.0 %all-gather.5.cloned.1.call-start = ((), (), s32[]{:S(2)}) async-start(), calls=%async_computation.3 | async-start | bytes 23592960 | tf_op jit(solution)/shard_map/all_gather | solution.py:76
  17.5 85.6 %all-to-all-start.1 = ((bf16[192,4,1024]{2,0,1:T(8,128)(2,1)}), bf16[192,4,1024]{2,0,1:T(8,128)(2,1)S(1)}, u32[]{:S(2)}, u32[]{:S(2)}) async-start(bf16[192,4,1024]{2,0,1:T(8,128)(2,1)} %copy.38), calls=%async_computation.1 | async-start | bytes 3145728 | tf_op jit(solution)/shard_map/all_to_all | solution.py:106
  23.9 638.8 %all-reduce.9.cloned.1.call-start = ((), (), s32[]{:S(2)}) async-start(), calls=%async_computation.5 | async-start | bytes 2228224 | tf_op jit(solution)/shard_map/psum | solution.py:134
  103.6 160.3 %copy-start.6 = (bf16[8192,16]{0,1:T(8,128)(2,1)S(1)}, bf16[8192,16]{0,1:T(8,128)(2,1)}, u32[]{:S(2)}) copy-start(bf16[8192,16]{0,1:T(8,128)(2,1)} %param.17) | copy-start | bytes 786436
  103.6 160.2 %copy-start.7 = (bf16[8192,16]{0,1:T(8,128)(2,1)S(1)}, bf16[8192,16]{0,1:T(8,128)(2,1)}, u32[]{:S(2)}) copy-start(bf16[8192,16]{0,1:T(8,128)(2,1)} %param.15) | copy-start | bytes 786436
  406.9 0.7 copy-start.9
  592.3 0.9 copy-start.2
  593.9 1.5 copy-start.5
  623.6 39.1 %copy-start.4 = (bf16[8,768,128]{2,1,0:T(8,128)(2,1)S(1)}, bf16[8,768,128]{2,1,0:T(8,128)(2,1)}, u32[]{:S(2)}) copy-start(bf16[8,768,128]{2,1,0:T(8,128)(2,1)} %get-tuple-element.648) | copy-start | bytes 4718596
  623.6 78.4 %all-reduce.7.cloned.1.call-start = ((), (), s32[]{:S(2)}) async-start(), calls=%async_computation.4 | async-start | bytes 2228224 | tf_op jit(solution)/shard_map/psum | solution.py:133
  665.8 41.4 %all-to-all-start = ((bf16[4,192,1024]{2,1,0:T(8,128)(2,1)}), bf16[4,192,1024]{2,1,0:T(8,128)(2,1)S(1)}, u32[]{:S(2)}, u32[]{:S(2)}) async-start(bf16[4,192,1024]{2,1,0:T(8,128)(2,1)} %all_to_all.24), calls=%async_computation | async-start | bytes 3145728 | tf_op jit(solution)/shard_map/all_to_all | solution.py:109
  708.4 2.4 copy-start.8
Sparse Core Ops, SparseCore 0:
  13.4 250.3 all-gather.2
  265.7 106.5 all-gather.4
  623.7 38.8 all-reduce.8
  665.0 36.9 all-reduce.6
